TPU v7x, 32 devices: a whole 2x2x4 slice. The times are simulated.
32 devices in a mesh: rep: 2 (over y), own: 16 (over z, x, core).
Axes of the slice: x: 2, y: 2, z: 4, core: 2. Of those that a mesh axis runs over, the one named last changes fastest.
Arguments:
- values: float32 [262144, 128], P(('rep', 'own')), may hold values from -0.8 to 0.8
- key_ids: int32 [262144], P(('rep', 'own')), may hold values from 0 to 65535, as said below
- heavy_ids: int32 [2048], replicated, may hold values from 0 to 65535, as said below
- block_offsets: int32 [32, 16], P(('rep', 'own')), may hold values from 0 to 8191, as said below
- block_counts: int32 [32, 16], P(('rep', 'own')), may hold values from 8 to 64, as said below
Outputs:
- light_sums: float32 [65536, 128], P('own')
- heavy_sums: float32 [2048, 128], P('own')
Inputs may be any that keep to these rules, and one draw needn't show every extreme that they name: `key_ids`: an event in block o of a device has a key in o * 4096 to (o + 1) * 4096 - 1 that is not a heavy key; every event outside all blocks has a heavy key. `heavy_ids`: distinct keys. `block_offsets`: on each device the blocks lie in the order of o, do not meet, and end by position 8192. `block_counts`: at most 64; one owner gets exactly 64 from every device.
All inputs are finite; a program needn't handle non-finite values.
Results may differ from a plain program's by a relative error of at most 0.000075.
Values sent between devices are 32-bit elements; how exact they have to be, the bound alone decides.
A program may use at most 64 MiB of HBM per device.

v0:
```python
import math
import jax
import jax.numpy as jnp
from jax import lax
from jax.sharding import PartitionSpec as P

KEYS_DEV = 4096
CAP = 64


def key_sums(rows_in, row_keys, targets):
    slots = row_keys.shape[0]
    block_len = math.gcd(slots, 2048)
    count_blocks = slots // block_len
    rows_blocks = rows_in.reshape(count_blocks, block_len, rows_in.shape[1])
    keys_blocks = row_keys.reshape(count_blocks, block_len)

    def accumulate(running, pieces):
        rows_piece, keys_piece = pieces
        onehot = (targets[:, None] == keys_piece[None, :]).astype(jnp.float32)
        added = jnp.dot(
            onehot, rows_piece, precision=lax.Precision.HIGHEST, preferred_element_type=jnp.float32
        )
        return (running + added, None)

    start_sums = jnp.zeros((targets.shape[0], rows_in.shape[1]), jnp.float32)
    running, unused = lax.scan(accumulate, start_sums, (rows_blocks, keys_blocks))
    return running


def per_device(values, key_ids, heavy_ids, block_offsets, block_counts):
    owners = lax.axis_size("own")
    pairs = lax.axis_size("rep")
    own_index = lax.axis_index("own")
    rep_index = lax.axis_index("rep")
    width = values.shape[1]
    slot_cap = CAP
    padded_values = jnp.concatenate([values, jnp.zeros((slot_cap, width), jnp.float32)], axis=0)
    padded_keys = jnp.concatenate([key_ids, jnp.full((slot_cap,), -1, jnp.int32)], axis=0)
    slot_iota = jnp.arange(slot_cap, dtype=jnp.int32)
    positions = block_offsets[0][:, None] + slot_iota[None, :]
    valid = slot_iota[None, :] < block_counts[0][:, None]
    block_rows = jnp.where(valid[:, :, None], jnp.take(padded_values, positions, axis=0), 0.0)
    block_keys = jnp.where(valid, jnp.take(padded_keys, positions, axis=0), -1)
    half_keys = KEYS_DEV // 2
    owner_base = (jnp.arange(owners, dtype=jnp.int32) * KEYS_DEV)[:, None]
    which_half = jnp.where(block_keys >= 0, (block_keys - owner_base) // half_keys, -1)
    split_rows = jnp.stack(
        [jnp.where((which_half == side)[:, :, None], block_rows, 0.0) for side in range(pairs)],
        axis=0,
    )
    split_keys = jnp.stack(
        [jnp.where(which_half == side, block_keys, -1) for side in range(pairs)], axis=0
    )
    split_rows = split_rows.reshape(pairs * owners, slot_cap, width)
    split_keys = split_keys.reshape(pairs * owners, slot_cap)
    got_rows, got_keys = (
        lax.all_to_all(split_rows, ("rep", "own"), split_axis=0, concat_axis=0, tiled=True),
        lax.all_to_all(split_keys, ("rep", "own"), split_axis=0, concat_axis=0, tiled=True),
    )
    local_keys = jnp.where(
        got_keys >= 0, got_keys - own_index * KEYS_DEV - rep_index * half_keys, -1
    ).reshape(-1)
    owned_half = key_sums(
        got_rows.reshape(-1, width), local_keys, jnp.arange(half_keys, dtype=jnp.int32)
    )
    light_sums = lax.all_gather(owned_half, "rep", axis=0, tiled=True)
    partial_sums = key_sums(values, key_ids, heavy_ids)
    summed_pair = lax.psum(partial_sums, "rep")
    heavy_sums = lax.psum_scatter(summed_pair, "own", scatter_dimension=0, tiled=True)
    return (light_sums, heavy_sums)


def solution(mesh):
    placed = (
        P(("rep", "own"), None),
        P(("rep", "own")),
        P(),
        P(("rep", "own"), None),
        P(("rep", "own"), None),
    )
    return jax.shard_map(
        per_device,
        mesh=mesh,
        in_specs=placed,
        out_specs=(P("own", None), P("own", None)),
        check_vma=False,
    )
```

profile of v0, /device:TPU:0, one launch (start us, length us, event | category | flops | bytes accessed | tf_op | source)
XLA Modules:
  0.0 166.0 jit_solution(6468750620577032743)
XLA Ops:
  8.0 0.7 compare_select_fusion.2
  8.7 0.1 reshape.548
  8.8 0.8 concatenate.6
  9.6 0.0 copy-start.3
  9.6 0.0 copy-start.4
  9.6 6.1 %gather_fusion = s32[1024]{0:T(1024)S(1)} fusion(s32[8256]{0:T(1024)S(1)} %concatenate.6, s32[1024]{0:T(1024)S(1)} %broadcast_clamp_fusion), kind=kCustom, calls=%fused_computation | custom fusion | bytes 12288 | tf_op jit(solution)/shard_map/jit(_take)/gather | solution.py:44
  15.7 0.1 gather.13
  15.8 0.0 copy-done.3
  15.8 0.0 copy-done.4
  15.8 0.1 compare_select_fusion.5
  15.9 0.6 pad_add_fusion
  16.5 7.3 %all-to-all-start = ((s32[32,1,64]{2,1,0:T(1,128)}), s32[32,1,64]{2,1,0:T(1,128)S(1)}, u32[]{:S(2)}, u32[]{:S(2)}) async-start(s32[32,1,64]{2,1,0:T(1,128)} %bitcast.2), calls=%async_computation | async-start | bytes 32768 | tf_op jit(solution)/shard_map/all_to_all | solution.py:59
  23.8 0.1 reshape.547
  23.9 3.7 %concatenate.7 = f32[8256,128]{1,0:T(8,128)} pad(f32[8192,128]{1,0:T(8,128)} %param.7, f32[]{:T(128)} %constant.82.clone.1), padding=0_64x0_0 | pad | bytes 8421380 | tf_op jit(solution)/shard_map/concatenate | solution.py:38
  27.6 0.0 copy-start.1
  27.6 0.0 copy-start.5
  27.6 5.0 %gather_fusion.1 = f32[1024,128]{1,0:T(8,128)S(1)} fusion(f32[8256,128]{1,0:T(8,128)} %concatenate.7, s32[1024]{0:T(1024)S(1)} %broadcast_clamp_fusion), kind=kCustom, calls=%fused_computation.1 | custom fusion | bytes 1052672 | tf_op jit(solution)/shard_map/jit(_take)/gather | solution.py:43
  32.6 0.1 broadcast_compare_fusion.1
  32.8 0.7 fusion.13
  33.5 1.1 pad_maximum_fusion
  34.6 0.0 copy-done.1
  34.6 0.0 all-to-all-done
  34.6 5.8 %all-to-all-start.1 = ((f32[32,64,128]{2,1,0:T(8,128)}), f32[32,64,128]{2,1,0:T(8,128)S(1)}, u32[]{:S(2)}, u32[]{:S(2)}) async-start(f32[32,64,128]{2,1,0:T(8,128)} %bitcast.4), calls=%async_computation.1 | async-start | bytes 2097152 | tf_op jit(solution)/shard_map/all_to_all | solution.py:58
  40.4 0.0 reduce-scatter.2.cloned.1.call-start
  40.5 0.0 copy-done.5
  40.5 34.5 %while.3 = (s32[]{:T(128)}, f32[2048,128]{1,0:T(8,128)S(1)}, s32[2048]{0:T(1024)S(1)}, s32[4,2048]{1,0:T(4,128)S(1)}, f32[4,2048,128]{2,1,0:T(8,128)}, /*index=5*/s32[]{:T(128)}, s32[]{:T(128)}) while((s32[]{:T(128)}, f32[2048,128]{1,0:T(8,128)S(1)}, s32[2048]{0:T(1024)S(1)}, s32[4,2048]{1,0:T(4,128)S(1)}, ...), condition=%wide.region_1.2_spmd.clone, body=%wide.region_0.1_spmd.clone.sunk | while | flops 6447169536 | bytes 3178599 | solution.py:27
  40.5 8.6 %fusion.34 = f32[2048,128]{1,0:T(8,128)S(1)} fusion(s32[2048]{0:T(1024)S(1)} %bitcast.21, s32[2048]{0:T(1024)S(1)} %get-tuple-element.128, f32[2048,128]{1,0:T(8,128)S(1)} %get-tuple-element.120, f32[4,2048,128]{2,1,0:T(8,128)} %get-tuple-element.130, s32[]{:T(128)S(6)} %copy.9, pred[]{:T(512)S(6)} %compare.29), kind=kOutput, calls=%fused_computation.6.clone.1 | convolution fusion | flops 6447169536 | bytes 3162117 | tf_op jit(solution)/shard_map/while/body/eval_jaxpr/dot_general | solution.py:21
  49.2 8.6 %fusion.34 = f32[2048,128]{1,0:T(8,128)S(1)} fusion(s32[2048]{0:T(1024)S(1)} %bitcast.21, s32[2048]{0:T(1024)S(1)} %get-tuple-element.128, f32[2048,128]{1,0:T(8,128)S(1)} %get-tuple-element.120, f32[4,2048,128]{2,1,0:T(8,128)} %get-tuple-element.130, s32[]{:T(128)S(6)} %copy.9, pred[]{:T(512)S(6)} %compare.29), kind=kOutput, calls=%fused_computation.6.clone.1 | convolution fusion | flops 6447169536 | bytes 3162117 | tf_op jit(solution)/shard_map/while/body/eval_jaxpr/dot_general | solution.py:21
  57.8 8.6 %fusion.34 = f32[2048,128]{1,0:T(8,128)S(1)} fusion(s32[2048]{0:T(1024)S(1)} %bitcast.21, s32[2048]{0:T(1024)S(1)} %get-tuple-element.128, f32[2048,128]{1,0:T(8,128)S(1)} %get-tuple-element.120, f32[4,2048,128]{2,1,0:T(8,128)} %get-tuple-element.130, s32[]{:T(128)S(6)} %copy.9, pred[]{:T(512)S(6)} %compare.29), kind=kOutput, calls=%fused_computation.6.clone.1 | convolution fusion | flops 6447169536 | bytes 3162117 | tf_op jit(solution)/shard_map/while/body/eval_jaxpr/dot_general | solution.py:21
  66.4 8.6 %fusion.34 = f32[2048,128]{1,0:T(8,128)S(1)} fusion(s32[2048]{0:T(1024)S(1)} %bitcast.21, s32[2048]{0:T(1024)S(1)} %get-tuple-element.128, f32[2048,128]{1,0:T(8,128)S(1)} %get-tuple-element.120, f32[4,2048,128]{2,1,0:T(8,128)} %get-tuple-element.130, s32[]{:T(128)S(6)} %copy.9, pred[]{:T(512)S(6)} %compare.29), kind=kOutput, calls=%fused_computation.6.clone.1 | convolution fusion | flops 6447169536 | bytes 3162117 | tf_op jit(solution)/shard_map/while/body/eval_jaxpr/dot_general | solution.py:21
  75.0 0.0 copy-start
  75.0 1.0 copy-done
  76.0 0.0 reduce-scatter.2.cloned.1.call-update
  76.0 0.2 all-gather.2.cloned.1.call-start
  76.2 0.1 fusion.14
  76.3 0.1 select_n.222
  76.4 0.0 all-to-all-done.1
  76.4 8.6 %fusion.10 = f32[2048,128]{1,0:T(8,128)} fusion(f32[2048,128]{1,0:T(8,128)S(1)} %bitcast.20, s32[2048]{0:T(1024)S(1)} %select_n.222), kind=kOutput, calls=%fused_computation.12 | convolution fusion | flops 6446645248 | bytes 2105344 | tf_op jit(solution)/shard_map/while/body/eval_jaxpr/dot_general | solution.py:21
  84.9 0.0 all-gather.2.cloned.1.call-update
  85.0 0.0 all-reduce.4.cloned.1.call-start
  85.0 50.0 %reduce-scatter.2.cloned.1.call-done = f32[128,128]{1,0:T(8,128)} async-done(((f32[2048,128]{1,0:T(8,128)}), f32[128,128]{1,0:T(8,128)}) %reduce-scatter.2.cloned.1.call-update) | async-done | bytes 65552 | tf_op jit(solution)/shard_map/reduce_scatter | solution.py:70
  135.0 0.0 all-reduce.4.cloned.1.call-update
  135.0 0.0 all-gather.2.cloned.1.call-done
  135.0 19.8 %all-reduce.4.cloned.1.call-done = f32[128,128]{1,0:T(8,128)} async-done(((f32[128,128]{1,0:T(8,128)}), f32[128,128]{1,0:T(8,128)}) %all-reduce.4.cloned.1.call-update) | async-done | bytes 65552 | tf_op jit(solution)/shard_map/psum | solution.py:69
  154.9 0.0 copy-start.2
  154.9 3.1 %copy.15 = f32[4096,128]{1,0:T(8,128)} copy(f32[4096,128]{1,0:T(8,128)} %all-gather.2.cloned.1.call-done) | data formatting | bytes 4194304
  157.9 0.0 copy-done.2
  157.9 0.6 copy.16
  (9 shorter events, 0.1 us)
Async XLA Ops:
  9.6 6.2 %copy-start.3 = (s32[1,16]{1,0:T(1,128)S(1)}, s32[1,16]{1,0:T(1,128)}, u32[]{:S(2)}) copy-start(s32[1,16]{1,0:T(1,128)} %param.10) | copy-start | bytes 196
  9.6 6.2 %copy-start.4 = (s32[1,16]{1,0:T(1,128)S(1)}, s32[1,16]{1,0:T(1,128)}, u32[]{:S(2)}) copy-start(s32[1,16]{1,0:T(1,128)} %param.11) | copy-start | bytes 196
  16.5 18.1 %all-to-all-start = ((s32[32,1,64]{2,1,0:T(1,128)}), s32[32,1,64]{2,1,0:T(1,128)S(1)}, u32[]{:S(2)}, u32[]{:S(2)}) async-start(s32[32,1,64]{2,1,0:T(1,128)} %bitcast.2), calls=%async_computation | async-start | bytes 32768 | tf_op jit(solution)/shard_map/all_to_all | solution.py:59
  27.6 6.9 %copy-start.1 = (s32[8192]{0:T(1024)S(1)}, s32[8192]{0:T(1024)}, u32[]{:S(2)}) copy-start(s32[8192]{0:T(1024)} %param.8) | copy-start | bytes 98308
  27.6 12.9 %copy-start.5 = (s32[2048]{0:T(1024)S(1)}, s32[2048]{0:T(1024)}, u32[]{:S(2)}) copy-start(s32[2048]{0:T(1024)} %param.9) | copy-start | bytes 24580
  34.6 41.8 %all-to-all-start.1 = ((f32[32,64,128]{2,1,0:T(8,128)}), f32[32,64,128]{2,1,0:T(8,128)S(1)}, u32[]{:S(2)}, u32[]{:S(2)}) async-start(f32[32,64,128]{2,1,0:T(8,128)} %bitcast.4), calls=%async_computation.1 | async-start | bytes 2097152 | tf_op jit(solution)/shard_map/all_to_all | solution.py:58
  40.4 94.5 %reduce-scatter.2.cloned.1.call-start = ((), (), s32[]{:S(2)}) async-start(), calls=%async_computation.4 | async-start | bytes 1114112 | tf_op jit(solution)/shard_map/reduce_scatter | solution.py:70
  75.0 1.0 copy-start
  76.0 59.1 %all-gather.2.cloned.1.call-start = ((), (), s32[]{:S(2)}) async-start(), calls=%async_computation.3 | async-start | bytes 3145728 | tf_op jit(solution)/shard_map/all_gather | solution.py:67
  85.0 69.9 %all-reduce.4.cloned.1.call-start = ((), (), s32[]{:S(2)}) async-start(), calls=%async_computation.5 | async-start | bytes 131072 | tf_op jit(solution)/shard_map/psum | solution.py:69
  154.9 3.1 %copy-start.2 = (f32[128,128]{1,0:T(8,128)S(1)}, f32[128,128]{1,0:T(8,128)}, u32[]{:S(2)}) copy-start(f32[128,128]{1,0:T(8,128)} %all-reduce.4.cloned.1.call-done) | copy-start | bytes 196612
Sparse Core Ops, SparseCore 0:
  76.1 58.8 reduce-scatter.1
Sparse Core Ops, SparseCore 1:
  85.0 34.2 all-gather.1
  135.1 19.7 all-reduce.3
where the time goes:
time: 167 us; the launch traced here: 166 us
  waiting for transfers between devices  69.9 us (42%)
  matrix products  42.9 us (26%)
  local copies, waits for them, and re-layouts  20.7 us (12%)
  between operations  15.6 us (9%)
  starting transfers between devices  13.5 us (8%)
  other arithmetic  3.39 us (2%)
    reduce_scatter x1, waiting for transfers between devices, per_device(): lax.psum_scatter(summed_pair, 'own', scatter_dimension=0, tiled=True)  50 us
    dot_general x5, matrix products, accumulate(): jnp.dot(onehot, rows_piece, precision=lax.Precision.HIGHEST, preferred_el...  42.9 us
    psum x1, waiting for transfers between devices, per_device(): summed_pair = lax.psum(partial_sums, 'rep')  19.8 us
    all_to_all x1, starting transfers between devices, per_device(): lax.all_to_all(split_keys, ('rep', 'own'), split_axis=0, concat_axis=0, t...  7.33 us
    gather x3, local copies, waits for them, and re-layouts, per_device(): block_keys = jnp.where(valid, jnp.take(padded_keys, positions, axis=0), -1)  6.28 us
    all_to_all x1, starting transfers between devices, per_device(): lax.all_to_all(split_rows, ('rep', 'own'), split_axis=0, concat_axis=0, t...  5.84 us
    gather x1, local copies, waits for them, and re-layouts, per_device(): jnp.take(padded_values, positions, axis=0)  5 us
    unnamed x14, local copies, waits for them, and re-layouts  4.68 us
  transfers between devices with their start and end apart: 5, of which 2 were waited for; matrix products, arithmetic and copies ran while one was open for 32% of the time, Pallas kernels for 0%

commit v1 on v0

--- a/solution.py
+++ b/solution.py
@@ -66,7 +66,7 @@
     )
     light_sums = lax.all_gather(owned_half, "rep", axis=0, tiled=True)
     partial_sums = key_sums(values, key_ids, heavy_ids)
-    summed_pair = lax.psum(partial_sums, "rep")
+    summed_pair = jnp.sum(lax.all_gather(partial_sums, "rep"), axis=0)
     heavy_sums = lax.psum_scatter(summed_pair, "own", scatter_dimension=0, tiled=True)
     return (light_sums, heavy_sums)
 

time: 167 us -> 217 us (1.30)
  waiting for transfers between devices: 69.9 us -> 120 us
  other arithmetic: 3.39 us -> 6.2 us
    all_gather x1, waiting for transfers between devices: 0.02 us -> 32.4 us  [per_device(): light_sums = lax.all_gather(owned_half, 'rep', axis=0, tiled=True)]
    all_gather x0 -> x1, waiting for transfers between devices: none -> 25.5 us  [per_device(): summed_pair = jnp.sum(lax.all_gather(partial_sums, 'rep'), axis=0)]
    psum x1 -> x0, waiting for transfers between devices: 19.8 us -> none  [per_device(): summed_pair = lax.psum(partial_sums, 'rep')]
    reduce_scatter x1, waiting for transfers between devices: 50 us -> 61.8 us  [per_device(): lax.psum_scatter(summed_pair, 'own', scatter_dimension=0, tiled=True)]
    reduce_sum x0 -> x1, other arithmetic: none -> 2.8 us  [per_device(): summed_pair = jnp.sum(lax.all_gather(partial_sums, 'rep'), axis=0)]
    unnamed x14 -> x11, local copies, waits for them, and re-layouts: 4.68 us -> 4.01 us
  transfers between devices with their start and end apart: 5 -> 5, of which waited for: 2 -> 3; matrix products, arithmetic and copies ran while one was open for 32% -> 26% of each run, Pallas kernels for 0% -> 0%
where the time goes in v1:
time: 217 us; the launch traced here: 216 us
  waiting for transfers between devices  120 us (55%)
  matrix products  42.9 us (20%)
  local copies, waits for them, and re-layouts  20 us (9%)
  between operations  13.9 us (6%)
  starting transfers between devices  13.5 us (6%)
  other arithmetic  6.2 us (3%)
    reduce_scatter x1, waiting for transfers between devices, per_device(): lax.psum_scatter(summed_pair, 'own', scatter_dimension=0, tiled=True)  61.8 us
    dot_general x5, matrix products, accumulate(): jnp.dot(onehot, rows_piece, precision=lax.Precision.HIGHEST, preferred_el...  42.9 us
    all_gather x1, waiting for transfers between devices, per_device(): light_sums = lax.all_gather(owned_half, 'rep', axis=0, tiled=True)  32.4 us
    all_gather x1, waiting for transfers between devices, per_device(): summed_pair = jnp.sum(lax.all_gather(partial_sums, 'rep'), axis=0)  25.5 us
    all_to_all x1, starting transfers between devices, per_device(): lax.all_to_all(split_keys, ('rep', 'own'), split_axis=0, concat_axis=0, t...  7.33 us
    gather x3, local copies, waits for them, and re-layouts, per_device(): block_keys = jnp.where(valid, jnp.take(padded_keys, positions, axis=0), -1)  6.28 us
    all_to_all x1, starting transfers between devices, per_device(): lax.all_to_all(split_rows, ('rep', 'own'), split_axis=0, concat_axis=0, t...  5.84 us
    gather x1, local copies, waits for them, and re-layouts, per_device(): jnp.take(padded_values, positions, axis=0)  5 us
  transfers between devices with their start and end apart: 5, of which 3 were waited for; matrix products, arithmetic and copies ran while one was open for 26% of the time, Pallas kernels for 0%

profile of v1, /device:TPU:0, one launch (start us, length us, event | category | flops | bytes accessed | tf_op | source)
XLA Modules:
  0.0 216.3 jit_solution(12231707512945634601)
XLA Ops:
  7.2 0.7 compare_select_fusion.2
  7.9 0.1 reshape.548
  8.0 0.8 concatenate.6
  8.7 0.0 copy-start.2
  8.7 0.0 copy-start.3
  8.8 6.1 %gather_fusion = s32[1024]{0:T(1024)S(1)} fusion(s32[8256]{0:T(1024)S(1)} %concatenate.6, s32[1024]{0:T(1024)S(1)} %broadcast_clamp_fusion), kind=kCustom, calls=%fused_computation | custom fusion | bytes 12288 | tf_op jit(solution)/shard_map/jit(_take)/gather | solution.py:44
  14.9 0.1 gather.13
  15.0 0.0 copy-done.2
  15.0 0.0 copy-done.3
  15.0 0.1 compare_select_fusion.5
  15.1 0.6 pad_add_fusion
  15.7 7.3 %all-to-all-start = ((s32[32,1,64]{2,1,0:T(1,128)}), s32[32,1,64]{2,1,0:T(1,128)S(1)}, u32[]{:S(2)}, u32[]{:S(2)}) async-start(s32[32,1,64]{2,1,0:T(1,128)} %bitcast.2), calls=%async_computation | async-start | bytes 32768 | tf_op jit(solution)/shard_map/all_to_all | solution.py:59
  23.0 0.1 reshape.547
  23.1 0.1 broadcast_compare_fusion.1
  23.2 3.7 %concatenate.7 = f32[8256,128]{1,0:T(8,128)} pad(f32[8192,128]{1,0:T(8,128)} %param.7, f32[]{:T(128)} %constant.82.clone.1), padding=0_64x0_0 | pad | bytes 8421380 | tf_op jit(solution)/shard_map/concatenate | solution.py:38
  26.9 0.0 copy-start.1
  26.9 0.0 copy-start.4
  26.9 5.0 %gather_fusion.1 = f32[1024,128]{1,0:T(8,128)S(1)} fusion(f32[8256,128]{1,0:T(8,128)} %concatenate.7, s32[1024]{0:T(1024)S(1)} %broadcast_clamp_fusion), kind=kCustom, calls=%fused_computation.1 | custom fusion | bytes 1052672 | tf_op jit(solution)/shard_map/jit(_take)/gather | solution.py:43
  31.9 0.7 fusion.13
  32.6 1.1 pad_maximum_fusion
  33.7 0.0 copy-done.1
  33.8 0.0 all-to-all-done
  33.8 5.8 %all-to-all-start.1 = ((f32[32,64,128]{2,1,0:T(8,128)}), f32[32,64,128]{2,1,0:T(8,128)S(1)}, u32[]{:S(2)}, u32[]{:S(2)}) async-start(f32[32,64,128]{2,1,0:T(8,128)} %bitcast.4), calls=%async_computation.1 | async-start | bytes 2097152 | tf_op jit(solution)/shard_map/all_to_all | solution.py:58
  39.6 0.0 all-gather.6.cloned.1.call-start
  39.7 0.0 copy-done.4
  39.7 34.5 %while.3 = (s32[]{:T(128)}, f32[2048,128]{1,0:T(8,128)S(1)}, s32[2048]{0:T(1024)S(1)}, s32[4,2048]{1,0:T(4,128)S(1)}, f32[4,2048,128]{2,1,0:T(8,128)}, /*index=5*/s32[]{:T(128)}, s32[]{:T(128)}) while((s32[]{:T(128)}, f32[2048,128]{1,0:T(8,128)S(1)}, s32[2048]{0:T(1024)S(1)}, s32[4,2048]{1,0:T(4,128)S(1)}, ...), condition=%wide.region_1.2_spmd.clone, body=%wide.region_0.1_spmd.clone.sunk | while | flops 6447169536 | bytes 3178599 | solution.py:27
  39.7 8.6 %fusion.34 = f32[2048,128]{1,0:T(8,128)S(1)} fusion(s32[2048]{0:T(1024)S(1)} %bitcast.23, s32[2048]{0:T(1024)S(1)} %get-tuple-element.128, f32[2048,128]{1,0:T(8,128)S(1)} %get-tuple-element.120, f32[4,2048,128]{2,1,0:T(8,128)} %get-tuple-element.130, s32[]{:T(128)S(6)} %copy.9, pred[]{:T(512)S(6)} %compare.29), kind=kOutput, calls=%fused_computation.6.clone.1 | convolution fusion | flops 6447169536 | bytes 3162117 | tf_op jit(solution)/shard_map/while/body/eval_jaxpr/dot_general | solution.py:21
  48.3 8.6 %fusion.34 = f32[2048,128]{1,0:T(8,128)S(1)} fusion(s32[2048]{0:T(1024)S(1)} %bitcast.23, s32[2048]{0:T(1024)S(1)} %get-tuple-element.128, f32[2048,128]{1,0:T(8,128)S(1)} %get-tuple-element.120, f32[4,2048,128]{2,1,0:T(8,128)} %get-tuple-element.130, s32[]{:T(128)S(6)} %copy.9, pred[]{:T(512)S(6)} %compare.29), kind=kOutput, calls=%fused_computation.6.clone.1 | convolution fusion | flops 6447169536 | bytes 3162117 | tf_op jit(solution)/shard_map/while/body/eval_jaxpr/dot_general | solution.py:21
  57.0 8.6 %fusion.34 = f32[2048,128]{1,0:T(8,128)S(1)} fusion(s32[2048]{0:T(1024)S(1)} %bitcast.23, s32[2048]{0:T(1024)S(1)} %get-tuple-element.128, f32[2048,128]{1,0:T(8,128)S(1)} %get-tuple-element.120, f32[4,2048,128]{2,1,0:T(8,128)} %get-tuple-element.130, s32[]{:T(128)S(6)} %copy.9, pred[]{:T(512)S(6)} %compare.29), kind=kOutput, calls=%fused_computation.6.clone.1 | convolution fusion | flops 6447169536 | bytes 3162117 | tf_op jit(solution)/shard_map/while/body/eval_jaxpr/dot_general | solution.py:21
  65.6 8.6 %fusion.34 = f32[2048,128]{1,0:T(8,128)S(1)} fusion(s32[2048]{0:T(1024)S(1)} %bitcast.23, s32[2048]{0:T(1024)S(1)} %get-tuple-element.128, f32[2048,128]{1,0:T(8,128)S(1)} %get-tuple-element.120, f32[4,2048,128]{2,1,0:T(8,128)} %get-tuple-element.130, s32[]{:T(128)S(6)} %copy.9, pred[]{:T(512)S(6)} %compare.29), kind=kOutput, calls=%fused_computation.6.clone.1 | convolution fusion | flops 6447169536 | bytes 3162117 | tf_op jit(solution)/shard_map/while/body/eval_jaxpr/dot_general | solution.py:21
  74.2 0.0 copy-start
  74.2 1.0 copy-done
  75.1 0.0 all-gather.6.cloned.1.call-update
  75.2 0.2 all-gather.4.cloned.1.call-start
  75.4 0.1 fusion.14
  75.5 0.1 select_n.222
  75.5 0.0 all-to-all-done.1
  75.5 8.6 %fusion.10 = f32[2048,128]{1,0:T(8,128)} fusion(f32[2048,128]{1,0:T(8,128)S(1)} %bitcast.22, s32[2048]{0:T(1024)S(1)} %select_n.222), kind=kOutput, calls=%fused_computation.12 | convolution fusion | flops 6446645248 | bytes 2105344 | tf_op jit(solution)/shard_map/while/body/eval_jaxpr/dot_general | solution.py:21
  84.1 0.0 all-gather.4.cloned.1.call-update
  84.1 0.0 reduce-scatter.2.cloned.1.call-start
  84.2 25.5 %all-gather.6.cloned.1.call-done = f32[4096,128]{1,0:T(8,128)} async-done(((f32[2048,128]{1,0:T(8,128)}), f32[4096,128]{1,0:T(8,128)}) %all-gather.6.cloned.1.call-update) | async-done | bytes 2097168 | tf_op jit(solution)/shard_map/all_gather | solution.py:69
  109.6 2.8 %reduce_sum.9 = f32[2048,128]{1,0:T(8,128)} reduce(f32[2,2048,128]{2,1,0:T(8,128)} %bitcast.21, f32[]{:T(128)} %constant.82.clone.1), dimensions={0}, to_apply=%region_2.3 | reduce | flops 262144 | bytes 3145732 | tf_op jit(solution)/shard_map/reduce_sum | solution.py:69
  112.4 0.0 reduce-scatter.2.cloned.1.call-update
  112.5 32.4 %all-gather.4.cloned.1.call-done = f32[4096,128]{1,0:T(8,128)} async-done(((f32[2048,128]{1,0:T(8,128)}), f32[4096,128]{1,0:T(8,128)}) %all-gather.4.cloned.1.call-update) | async-done | bytes 2097168 | tf_op jit(solution)/shard_map/all_gather | solution.py:67
  144.9 61.8 %reduce-scatter.2.cloned.1.call-done = f32[128,128]{1,0:T(8,128)} async-done(((f32[2048,128]{1,0:T(8,128)}), f32[128,128]{1,0:T(8,128)}) %reduce-scatter.2.cloned.1.call-update) | async-done | bytes 65552 | tf_op jit(solution)/shard_map/reduce_scatter | solution.py:70
  206.7 3.0 %copy.14 = f32[4096,128]{1,0:T(8,128)} copy(f32[4096,128]{1,0:T(8,128)} %all-gather.4.cloned.1.call-done) | data formatting | bytes 4194304
  (9 shorter events, 0.1 us)
Async XLA Ops:
  8.7 6.2 %copy-start.2 = (s32[1,16]{1,0:T(1,128)S(1)}, s32[1,16]{1,0:T(1,128)}, u32[]{:S(2)}) copy-start(s32[1,16]{1,0:T(1,128)} %param.10) | copy-start | bytes 196
  8.7 6.2 %copy-start.3 = (s32[1,16]{1,0:T(1,128)S(1)}, s32[1,16]{1,0:T(1,128)}, u32[]{:S(2)}) copy-start(s32[1,16]{1,0:T(1,128)} %param.11) | copy-start | bytes 196
  15.7 18.1 %all-to-all-start = ((s32[32,1,64]{2,1,0:T(1,128)}), s32[32,1,64]{2,1,0:T(1,128)S(1)}, u32[]{:S(2)}, u32[]{:S(2)}) async-start(s32[32,1,64]{2,1,0:T(1,128)} %bitcast.2), calls=%async_computation | async-start | bytes 32768 | tf_op jit(solution)/shard_map/all_to_all | solution.py:59
  26.9 6.8 %copy-start.1 = (s32[8192]{0:T(1024)S(1)}, s32[8192]{0:T(1024)}, u32[]{:S(2)}) copy-start(s32[8192]{0:T(1024)} %param.8) | copy-start | bytes 98308
  26.9 12.8 %copy-start.4 = (s32[2048]{0:T(1024)S(1)}, s32[2048]{0:T(1024)}, u32[]{:S(2)}) copy-start(s32[2048]{0:T(1024)} %param.9) | copy-start | bytes 24580
  33.8 41.8 %all-to-all-start.1 = ((f32[32,64,128]{2,1,0:T(8,128)}), f32[32,64,128]{2,1,0:T(8,128)S(1)}, u32[]{:S(2)}, u32[]{:S(2)}) async-start(f32[32,64,128]{2,1,0:T(8,128)} %bitcast.4), calls=%async_computation.1 | async-start | bytes 2097152 | tf_op jit(solution)/shard_map/all_to_all | solution.py:58
  39.6 70.0 %all-gather.6.cloned.1.call-start = ((), (), s32[]{:S(2)}) async-start(), calls=%async_computation.5 | async-start | bytes 3145728 | tf_op jit(solution)/shard_map/all_gather | solution.py:69
  74.2 1.0 copy-start
  75.2 69.7 %all-gather.4.cloned.1.call-start = ((), (), s32[]{:S(2)}) async-start(), calls=%async_computation.3 | async-start | bytes 3145728 | tf_op jit(solution)/shard_map/all_gather | solution.py:67
  84.1 122.6 %reduce-scatter.2.cloned.1.call-start = ((), (), s32[]{:S(2)}) async-start(), calls=%async_computation.4 | async-start | bytes 1114112 | tf_op jit(solution)/shard_map/reduce_scatter | solution.py:70
Sparse Core Ops, SparseCore 0:
  75.3 34.3 all-gather.5
  111.8 33.0 all-gather.3
  149.1 57.5 reduce-scatter.1
